TPU v7x, 32 devices: a whole 2x2x4 slice. The times are simulated.
32 devices in a mesh: groups: 2 (over x), blk: 16 (over z, y, core).
Axes of the slice: x: 2, y: 2, z: 4, core: 2. Of those that a mesh axis runs over, the one named last changes fastest.
Arguments:
- pair_elements: float32 [12288, 1024], P(('groups', 'blk')), parts along dimension 0, may hold values from -0.8 to 0.8
- gmap: int32 [12288], P(('groups', 'blk')), parts along dimension 0, may hold values from 0 to 6143, as said below
- w_screened: float32 [12288, 6144], P('groups', 'blk'), parts along dimension 0, as said below
- coulomb: float32 [12288], P(('groups', 'blk')), parts along dimension 0, may hold values from 0.001 to 0.02
Outputs:
- screened: float32 [12288, 1024], P(('groups', 'blk')), parts along dimension 0
- pair_sigma: float32 [2048], P(('groups', 'blk')), parts along dimension 0
There are 2 independent parts, one for each index of `groups`. A program takes and returns all parts, laid end to end along the dimension named above; each array names one. Nothing has to cross between parts.
Inputs may be any that keep to these rules, and one draw needn't show every extreme that they name: `gmap`: each aligned block of 384 entries is a permutation of that block's own indices. `w_screened`: symmetric.
All inputs are finite; a program needn't handle non-finite values.
Results may differ from a plain program's by a relative error of at most 0.00013.
Values sent between devices are 32-bit elements; how exact they have to be, the bound alone decides.
A program may use at most 256 MiB of HBM per device.

v0:
```python
import jax
import jax.numpy as jnp
from jax import lax
from jax.sharding import PartitionSpec as P

NB = 64
OCC = 4


def local(pair_elements, gmap, w_screened, coulomb):
    rows_here = pair_elements.shape[0]
    local_rows = gmap % rows_here
    elements = jnp.take(pair_elements, local_rows, axis=0)
    screened = lax.dot_general(
        w_screened,
        lax.all_gather(elements, "blk", axis=0, tiled=True),
        (((0,), (0,)), ((), ())),
        precision=lax.Precision.HIGHEST,
        preferred_element_type=jnp.float32,
    )
    band = jnp.arange(elements.shape[1], dtype=jnp.int32) % NB
    coef = jnp.where(band < OCC, -0.5, 0.5).astype(jnp.float32)
    partial_terms = coef * jnp.sum(screened * elements, axis=0) - 0.5 * jnp.sum(
        coulomb[:, None] * elements * elements, axis=0
    )
    pair_sigma = lax.psum_scatter(partial_terms, "blk", scatter_dimension=0, tiled=True)
    return (screened, pair_sigma)


def solution(mesh):
    in_specs = (
        P(("groups", "blk"), None),
        P(("groups", "blk")),
        P("groups", "blk"),
        P(("groups", "blk")),
    )
    out_specs = (P(("groups", "blk"), None), P(("groups", "blk")))
    return jax.shard_map(local, mesh=mesh, in_specs=in_specs, out_specs=out_specs, check_vma=False)
```

profile of v0, /device:TPU:0, one launch (start us, length us, event | category | flops | bytes accessed | tf_op | source)
XLA Modules:
  0.0 219.3 jit_solution(7147014922717818531)
XLA Ops:
  7.2 0.0 copy-start
  7.2 0.0 all-gather.2.cloned.1.call-start
  7.2 0.8 compare_and_fusion
  8.0 0.5 copy-done
  8.6 1.8 gather_fusion
  10.4 1.3 broadcast_select_fusion
  11.7 0.0 copy-start.3
  11.7 0.0 copy-start.1
  11.7 0.0 copy-start.2
  11.7 0.0 all-gather.2.cloned.1.call-update
  11.8 0.6 copy-done.3
  12.4 0.6 dynamic-slice
  13.6 129.5 %all-gather.2.cloned.1.call-done = f32[6144,1024]{1,0:T(8,128)} async-done(((f32[384,1024]{1,0:T(8,128)}), f32[6144,1024]{1,0:T(8,128)}) %all-gather.2.cloned.1.call-update) | async-done | bytes 25165840 | tf_op jit(solution)/shard_map/all_gather | solution.py:16
  143.2 0.0 copy-done.1
  143.2 0.0 copy-done.2
  143.2 36.1 %multiply_reduce_fusion = (f32[1024]{0:T(1024)S(1)}, f32[1024]{0:T(1024)S(1)}, f32[384,1024]{1,0:T(8,128)}) fusion(f32[384,1024]{1,0:T(8,128)S(1)} %copy-done.1, f32[384]{0:T(512)S(1)} %copy-done.2, f32[6144,1024]{1,0:T(8,128)} %all-gather.2.cloned.1.call-done, f32[6144,384]{1,0:T(8,128)} %param.6), kind=kOutput, calls=%fused_computation.3 | convolution fusion | flops 28992993280 | bytes 37758464 | tf_op jit(solution)/shard_map/dot_general | solution.py:14
  179.3 32.6 %all-reduce = f32[1024]{0:T(1024)S(1)} all-reduce(f32[1024]{0:T(1024)S(1)} %multiply_subtract_fusion), channel_id=2, replica_groups=mesh['groups'=2,'blk'=16] {'blk'}, use_global_device_ids=true, to_apply=%region_2.3.clone | all-reduce | flops 1024 | bytes 8192
  211.9 0.6 dynamic-slice.1
  (2 shorter events, 0.0 us)
Async XLA Ops:
  7.2 1.4 copy-start
  7.2 136.0 %all-gather.2.cloned.1.call-start = ((), (), s32[]{:S(2)}) async-start(), calls=%async_computation | async-start | bytes 26738688 | tf_op jit(solution)/shard_map/all_gather | solution.py:16
  11.7 0.7 copy-start.3
  11.7 131.4 %copy-start.1 = (f32[384,1024]{1,0:T(8,128)S(1)}, f32[384,1024]{1,0:T(8,128)}, u32[]{:S(2)}) copy-start(f32[384,1024]{1,0:T(8,128)} %broadcast_select_fusion) | copy-start | bytes 4718596
  11.7 131.4 %copy-start.2 = (f32[384]{0:T(512)S(1)}, f32[384]{0:T(512)}, u32[]{:S(2)}) copy-start(f32[384]{0:T(512)} %param.7) | copy-start | bytes 4612
Sparse Core Ops, SparseCore 0:
  11.9 131.2 all-gather.1
where the time goes:
time: 220 us; the launch traced here: 219 us
  waiting for transfers between devices  130 us (59%)
  matrix products  36.1 us (16%)
  blocking collectives  32.6 us (15%)
  between operations  14.7 us (7%)
  local copies, waits for them, and re-layouts  4.17 us (2%)
    all_gather x1, waiting for transfers between devices, local(): lax.all_gather(elements, 'blk', axis=0, tiled=True)  130 us
    dot_general x1, matrix products, local(): lax.dot_general(w_screened, lax.all_gather(elements, 'blk', axis=0, tiled...  36.1 us
    unnamed x1, blocking collectives  32.6 us
  transfers between devices with their start and end apart: 1, of which 1 were waited for; matrix products, arithmetic and copies ran while one was open for 0% of the time, Pallas kernels for 0%

commit v1 on v0

v1 whole, which is shorter than its diff:
```python
import functools

import jax
import jax.numpy as jnp
from jax import lax
from jax.experimental import pallas as pl
from jax.experimental.pallas import tpu as pltpu
from jax.sharding import PartitionSpec as P

NB = 64
OCC = 4
ROWS_Y = 2
CORES = 2
CHUNKS = 6
VMEM_ROOM = 58 * 2**20


def dot3(w, e):
    wt = w.T
    wh = wt.astype(jnp.bfloat16)
    wl = (wt - wh.astype(jnp.float32)).astype(jnp.bfloat16)
    eh = e.astype(jnp.bfloat16)
    el = (e - eh.astype(jnp.float32)).astype(jnp.bfloat16)
    dot = functools.partial(jnp.dot, preferred_element_type=jnp.float32)
    return dot(wl, eh) + dot(wh, el) + dot(wh, eh)


def kernel(depth, e_hbm, w_hbm, c_ref, out_ref, sig_ref, ez, ey, wbuf, parts, load_sem, s_y, s_up, s_dn, s_d2d, r_sem, p_send, p_recv):
    n = depth * ROWS_Y * CORES
    me = lax.axis_index("blk")
    z = me // (ROWS_Y * CORES)
    y = (me // CORES) % ROWS_Y
    c = me % CORES
    oy, oc = 1 - y, 1 - c
    head = ey.shape[1]
    body_rows = ez.shape[1]
    cols = ez.shape[2]

    def blk(zz, yy, cc):
        return (zz * ROWS_Y + yy) * CORES + cc

    own_y = pltpu.make_async_copy(e_hbm.at[pl.ds(0, head)], ey.at[me], load_sem.at[0])
    own_z = pltpu.make_async_copy(e_hbm.at[pl.ds(head, body_rows)], ez.at[me], load_sem.at[1])
    w_in = pltpu.make_async_copy(w_hbm, wbuf, load_sem.at[2])
    own_y.start()
    own_z.start()
    w_in.start()

    barrier = pltpu.get_barrier_semaphore()

    @pl.loop(1, n)
    def _(j):
        pl.semaphore_signal(barrier, inc=1, device_id={"blk": (me + j) % n}, device_id_type=pl.DeviceIdType.MESH)

    pl.semaphore_wait(barrier, n - 1)
    own_y.wait()
    own_z.wait()

    def piece(b, k):
        return ez.at[b, pl.ds(pl.multiple_of((k - 1) * head, head), head)]

    def rdma(ref, send, b, k, target):
        return pltpu.make_async_remote_copy(
            src_ref=ref, dst_ref=ref, send_sem=send, recv_sem=r_sem.at[b, k],
            device_id={"blk": target}, device_id_type=pl.DeviceIdType.MESH)

    def copy(kind, b, k, ref):
        zz, yy = b // (ROWS_Y * CORES), (b // CORES) % ROWS_Y
        if kind == "y":
            return rdma(ref, s_y.at[zz, k], b, k, blk(z, oy, c))
        if kind == "up":
            return rdma(ref, s_up.at[b // CORES, k], b, k, blk((z + 1) % depth, y, c))
        if kind == "dn":
            return rdma(ref, s_dn.at[b // CORES, k], b, k, blk((z + depth - 1) % depth, y, c))
        return rdma(ref, s_d2d.at[b // CORES, k], b, k, blk(z, y, oc))

    def landed(b, k, ref):
        rdma(ref, s_y.at[0, 0], b, k, blk(z, y, oc)).wait_recv()

    copy("y", me, 0, ey.at[me]).start()

    @pl.loop(1, CHUNKS)
    def _(k):
        @pl.when(z > 0)
        def _():
            copy("dn", me, k, piece(me, k)).start()

        @pl.when(z < depth - 1)
        def _():
            copy("up", me, k, piece(me, k)).start()

        copy("y", me, k, piece(me, k)).start()
        copy("d2d", me, k, piece(me, k)).start()

    copy("d2d", me, 0, ey.at[me]).start()
    out_ref[...] = jnp.zeros_like(out_ref)
    w_in.wait()

    other = blk(z, oy, c)
    landed(other, 0, ey.at[other])
    copy("d2d", other, 0, ey.at[other]).start()

    @pl.loop(0, depth + 1)
    def _(d):
        @pl.when(jnp.logical_and(d >= 1, d < depth))
        def _():
            @pl.loop(1, CHUNKS)
            def _(k):
                @pl.when(z + d < depth)
                def _():
                    b = blk((z + d) % depth, y, c)
                    landed(b, k, piece(b, k))

                    @pl.when(z > 0)
                    def _():
                        copy("dn", b, k, piece(b, k)).start()

                    copy("y", b, k, piece(b, k)).start()
                    copy("d2d", b, k, piece(b, k)).start()

                @pl.when(z - d >= 0)
                def _():
                    b = blk((z - d + depth) % depth, y, c)
                    landed(b, k, piece(b, k))

                    @pl.when(z < depth - 1)
                    def _():
                        copy("up", b, k, piece(b, k)).start()

                    copy("y", b, k, piece(b, k)).start()
                    copy("d2d", b, k, piece(b, k)).start()

        @pl.when(jnp.logical_and(z + d == depth - 1, z > 0))
        def _():
            copy("dn", me, 0, ey.at[me]).start()
            copy("dn", other, 0, ey.at[other]).start()

        @pl.when(jnp.logical_and(z - d == 0, z < depth - 1))
        def _():
            copy("up", me, 0, ey.at[me]).start()
            copy("up", other, 0, ey.at[other]).start()

        @pl.loop(0, 8)
        def _(i):
            cross = i // 4
            sign = (i // 2) % 2
            far = i % 2
            dist = d - cross
            zz = z + (2 * sign - 1) * dist
            ok = jnp.logical_and(dist >= 0, jnp.logical_or(sign == 0, dist > 0))
            ok = jnp.logical_and(ok, jnp.logical_and(zz >= 0, zz < depth))

            @pl.when(ok)
            def _():
                at = (zz + 2 * depth) % depth
                yy = (y + cross) % ROWS_Y
                cc = (c + far) % CORES
                b = blk(at, yy, cc)

                @pl.when(far == 1)
                def _():
                    @pl.loop(1, CHUNKS)
                    def _(k):
                        landed(b, k, piece(b, k))

                @pl.when(jnp.logical_and(far == 0, cross == 1))
                def _():
                    @pl.loop(1, CHUNKS)
                    def _(k):
                        landed(b, k, piece(b, k))
                        copy("d2d", b, k, piece(b, k)).start()

                out_ref[...] += dot3(wbuf[b, head:, :], ez[b])

    def first_pieces(zz):
        rows = ROWS_Y * CORES * head
        w = wbuf[pl.ds(zz * ROWS_Y * CORES, ROWS_Y * CORES), :head, :].reshape(rows, wbuf.shape[2])
        e = ey[pl.ds(zz * ROWS_Y * CORES, ROWS_Y * CORES)].reshape(rows, cols)
        out_ref[...] += dot3(w, e)

    @pl.loop(0, depth)
    def _(d):
        @pl.loop(0, 2)
        def _(sign):
            zz = z + (2 * sign - 1) * d
            ok = jnp.logical_and(jnp.logical_or(sign == 0, d > 0), jnp.logical_and(zz >= 0, zz < depth))

            @pl.when(ok)
            def _():
                at = (zz + depth) % depth

                @pl.when(d > 0)
                def _():
                    @pl.loop(0, ROWS_Y)
                    def _(j):
                        b = blk(at, (y + j) % ROWS_Y, c)
                        landed(b, 0, ey.at[b])

                        @pl.when(jnp.logical_and(sign == 1, z > 0))
                        def _():
                            copy("dn", b, 0, ey.at[b]).start()

                        @pl.when(jnp.logical_and(sign == 0, z < depth - 1))
                        def _():
                            copy("up", b, 0, ey.at[b]).start()

                        copy("d2d", b, 0, ey.at[b]).start()

                @pl.loop(0, ROWS_Y)
                def _(yy):
                    b = blk(at, yy, oc)
                    landed(b, 0, ey.at[b])

                first_pieces(at)

    own_head, own_body = ey[me], ez[me]
    coul = jnp.broadcast_to(c_ref[...], (128, c_ref.shape[1])).T[:, :1]
    band = lax.broadcasted_iota(jnp.int32, (1, cols), 1) % NB
    coef = jnp.where(band < OCC, -0.5, 0.5).astype(jnp.float32)
    screened_sum = jnp.sum(out_ref[:head, :] * own_head, axis=0, keepdims=True) + jnp.sum(
        out_ref[head:, :] * own_body, axis=0, keepdims=True)
    bare_sum = jnp.sum(coul[:head] * own_head * own_head, axis=0, keepdims=True) + jnp.sum(
        coul[head:] * own_body * own_body, axis=0, keepdims=True)
    parts[me] = coef * screened_sum - 0.5 * bare_sum

    def part_copy(source, target, j):
        return pltpu.make_async_remote_copy(
            src_ref=parts.at[source], dst_ref=parts.at[source], send_sem=p_send.at[j], recv_sem=p_recv.at[source],
            device_id={"blk": target}, device_id_type=pl.DeviceIdType.MESH)

    @pl.loop(1, n)
    def _(j):
        part_copy(me, (me + j) % n, j).start()

    @pl.loop(1, n)
    def _(j):
        part_copy((me + j) % n, (me + j) % n, j).wait_recv()

    sig_ref[...] = jnp.sum(parts[...], axis=0)

    @pl.loop(1, n)
    def _(j):
        part_copy(me, (me + j) % n, j).wait_send()

    @pl.loop(0, n // CORES)
    def _(h):
        zz, yy = h // ROWS_Y, h % ROWS_Y
        b = h * CORES + c

        def sent(kind, k, ref):
            copy(kind, b, k, ref).wait_send()

        @pl.loop(1, CHUNKS)
        def _(k):
            sent("d2d", k, piece(b, k))

            @pl.when(yy == y)
            def _():
                sent("y", k, piece(b, k))

                @pl.when(jnp.logical_and(zz >= z, z > 0))
                def _():
                    sent("dn", k, piece(b, k))

                @pl.when(jnp.logical_and(zz <= z, z < depth - 1))
                def _():
                    sent("up", k, piece(b, k))

        sent("d2d", 0, ey.at[b])

        @pl.when(b == me)
        def _():
            sent("y", 0, ey.at[b])

        @pl.when(jnp.logical_and(zz >= z, z > 0))
        def _():
            sent("dn", 0, ey.at[b])

        @pl.when(jnp.logical_and(zz <= z, z < depth - 1))
        def _():
            sent("up", 0, ey.at[b])


def fused(n, elements, w_screened, coulomb):
    rows, cols = elements.shape
    head = rows // CHUNKS
    depth = n // (ROWS_Y * CORES)
    f32 = jnp.float32
    half = n // CORES
    dma = pltpu.SemaphoreType.DMA
    screened, sig = pl.pallas_call(
        functools.partial(kernel, depth),
        out_shape=(jax.ShapeDtypeStruct((rows, cols), f32), jax.ShapeDtypeStruct((1, cols), f32)),
        in_specs=[pl.BlockSpec(memory_space=pl.ANY), pl.BlockSpec(memory_space=pl.ANY), pl.BlockSpec(memory_space=pltpu.VMEM)],
        out_specs=(pl.BlockSpec(memory_space=pltpu.VMEM), pl.BlockSpec(memory_space=pltpu.VMEM)),
        scratch_shapes=[
            pltpu.VMEM((n, rows - head, cols), f32),
            pltpu.VMEM((n, head, cols), f32),
            pltpu.VMEM((n, rows, rows), f32),
            pltpu.VMEM((n, 1, cols), f32),
            dma((3,)),
            dma((depth, CHUNKS)),
            dma((half, CHUNKS)),
            dma((half, CHUNKS)),
            dma((half, CHUNKS)),
            dma((n, CHUNKS)),
            dma((n,)),
            dma((n,)),
        ],
        compiler_params=pltpu.CompilerParams(collective_id=0, has_side_effects=True, vmem_limit_bytes=60 * 2**20),
        name="gather_matmul",
    )(elements, w_screened.reshape(n, rows, rows), coulomb.reshape(1, rows))
    me = lax.axis_index("blk")
    pair_sigma = lax.dynamic_slice(sig.reshape(cols), (me * (cols // n),), (cols // n,))
    return screened, pair_sigma


def plain(elements, w_screened, coulomb):
    screened = lax.dot_general(
        w_screened,
        lax.all_gather(elements, "blk", axis=0, tiled=True),
        (((0,), (0,)), ((), ())),
        precision=lax.Precision.HIGHEST,
        preferred_element_type=jnp.float32,
    )
    band = jnp.arange(elements.shape[1], dtype=jnp.int32) % NB
    coef = jnp.where(band < OCC, -0.5, 0.5).astype(jnp.float32)
    partial_terms = coef * jnp.sum(screened * elements, axis=0) - 0.5 * jnp.sum(
        coulomb[:, None] * elements * elements, axis=0
    )
    pair_sigma = lax.psum_scatter(partial_terms, "blk", scatter_dimension=0, tiled=True)
    return screened, pair_sigma


def solution(mesh):
    n = mesh.shape["blk"]

    def local(pair_elements, gmap, w_screened, coulomb):
        rows, cols = pair_elements.shape
        elements = jnp.take(pair_elements, gmap % rows, axis=0, mode="clip")
        held = 4 * n * rows * (cols + rows) + 4 * 3 * rows * cols
        fits = held < VMEM_ROOM and n % (ROWS_Y * CORES) == 0 and rows % (8 * CHUNKS) == 0
        if fits:
            return fused(n, elements, w_screened, coulomb)
        return plain(elements, w_screened, coulomb)

    in_specs = (
        P(("groups", "blk"), None),
        P(("groups", "blk")),
        P("groups", "blk"),
        P(("groups", "blk")),
    )
    out_specs = (P(("groups", "blk"), None), P(("groups", "blk")))
    return jax.shard_map(local, mesh=mesh, in_specs=in_specs, out_specs=out_specs, check_vma=False)
```

time: 220 us -> 178 us (0.81)
  Pallas kernels: 0 us -> 168 us
  waiting for transfers between devices: 130 us -> 0 us
  matrix products: 36.1 us -> 0 us
  blocking collectives: 32.6 us -> 0 us
  between operations: 14.7 us -> 0.65 us
  local copies, waits for them, and re-layouts: 4.17 us -> 7.64 us
    pallas_call x0 -> x1, Pallas kernels: none -> 168 us  [fused(): pl.pallas_call(functools.partial(kernel, depth), out_shape=(jax.ShapeDtyp...]
    all_gather x1 -> x0, waiting for transfers between devices: 130 us -> none  [local(): lax.all_gather(elements, 'blk', axis=0, tiled=True)]
    dot_general x1 -> x0, matrix products: 36.1 us -> none  [local(): lax.dot_general(w_screened, lax.all_gather(elements, 'blk', axis=0, tiled...]
    unnamed x1 -> x0, blocking collectives: 32.6 us -> none
  transfers between devices with their start and end apart: 1 -> 0, of which waited for: 1 -> 0; matrix products, arithmetic and copies ran while one was open for 0% -> 0% of each run, Pallas kernels for 0% -> 0%
where the time goes in v1:
time: 178 us; the launch traced here: 177 us
  Pallas kernels  168 us (94%)
  local copies, waits for them, and re-layouts  7.64 us (4%)
    pallas_call x1, Pallas kernels, fused(): pl.pallas_call(functools.partial(kernel, depth), out_shape=(jax.ShapeDtyp...  168 us

profile of v1, /device:TPU:0, one launch (start us, length us, event | category | flops | bytes accessed | tf_op | source)
XLA Modules:
  0.0 177.5 jit_solution(9284785022398802173)
XLA Ops:
  0.6 0.0 copy-start
  0.6 0.8 add_select_fusion
  1.5 0.6 copy-done
  2.1 0.0 copy-start.1
  2.1 2.5 %gather_fusion = f32[384,1024]{1,0:T(8,128)} fusion(f32[384,1024]{1,0:T(8,128)S(1)} %copy-done, s32[1024]{0:T(1024)S(1)} %pad_clamp_fusion), kind=kCustom, calls=%fused_computation | custom fusion | bytes 3147264 | tf_op jit(solution)/shard_map/jit(_take)/gather | solution.py:340
  4.5 0.0 copy-done.1
  4.5 0.6 reshape.13.c_ref
  5.1 168.3 %gather_matmul.1 = (f32[384,1024]{1,0:T(8,128)}, f32[1,1024]{1,0:T(1,128)}) custom-call(f32[384,1024]{1,0:T(8,128)} %gather_fusion, f32[16,384,384]{2,1,0:T(8,128)} %bitcast.3, f32[1,384]{1,0:T(1,128)} %reshape.13.c_ref), custom_call_target="tpu_custom_call" | custom-call | tf_op jit(solution)/shard_map/gather_matmul/pallas_call | solution.py:291
  173.5 1.3 dynamic-slice_bitcast_fusion
  174.7 2.7 %copy.7 = f32[384,1024]{1,0:T(8,128)} copy(f32[384,1024]{1,0:T(8,128)} %get-tuple-element.8) | data formatting | bytes 3145728
  (1 shorter events, 0.0 us)
Async XLA Ops:
  0.6 1.4 copy-start
  2.1 2.5 %copy-start.1 = (f32[384]{0:T(512)S(1)}, f32[384]{0:T(512)}, u32[]{:S(2)}) copy-start(f32[384]{0:T(512)} %param.7) | copy-start | bytes 4612

commit v2 on v1

--- a/solution.py
+++ b/solution.py
@@ -11,7 +11,7 @@
 OCC = 4
 ROWS_Y = 2
 CORES = 2
-CHUNKS = 6
+CHUNKS = 4
 VMEM_ROOM = 58 * 2**20
 
 
@@ -34,6 +34,7 @@
     oy, oc = 1 - y, 1 - c
     head = ey.shape[1]
     body_rows = ez.shape[1]
+    step = body_rows // (CHUNKS - 1)
     cols = ez.shape[2]
 
     def blk(zz, yy, cc):
@@ -57,7 +58,7 @@
     own_z.wait()
 
     def piece(b, k):
-        return ez.at[b, pl.ds(pl.multiple_of((k - 1) * head, head), head)]
+        return ez.at[b, pl.ds(pl.multiple_of((k - 1) * step, step), step)]
 
     def rdma(ref, send, b, k, target):
         return pltpu.make_async_remote_copy(
@@ -90,16 +91,29 @@
             copy("up", me, k, piece(me, k)).start()
 
         copy("y", me, k, piece(me, k)).start()
-        copy("d2d", me, k, piece(me, k)).start()
-
-    copy("d2d", me, 0, ey.at[me]).start()
+
     out_ref[...] = jnp.zeros_like(out_ref)
     w_in.wait()
+
+    @pl.loop(1, CHUNKS)
+    def _(k):
+        copy("d2d", me, k, piece(me, k)).start()
+
+    copy("d2d", me, 0, ey.at[me]).start()
 
     other = blk(z, oy, c)
     landed(other, 0, ey.at[other])
     copy("d2d", other, 0, ey.at[other]).start()
 
+    def pass_first(at, kind):
+        @pl.loop(0, ROWS_Y)
+        def _(j):
+            b = blk(at, (y + j) % ROWS_Y, c)
+            landed(b, 0, ey.at[b])
+            if kind is not None:
+                copy(kind, b, 0, ey.at[b]).start()
+            copy("d2d", b, 0, ey.at[b]).start()
+
     @pl.loop(0, depth + 1)
     def _(d):
         @pl.when(jnp.logical_and(d >= 1, d < depth))
@@ -135,10 +149,18 @@
             copy("dn", me, 0, ey.at[me]).start()
             copy("dn", other, 0, ey.at[other]).start()
 
+            @pl.loop(1, d + 1)
+            def _(j):
+                pass_first((z + j) % depth, "dn")
+
         @pl.when(jnp.logical_and(z - d == 0, z < depth - 1))
         def _():
             copy("up", me, 0, ey.at[me]).start()
             copy("up", other, 0, ey.at[other]).start()
+
+            @pl.loop(1, d + 1)
+            def _(j):
+                pass_first((z - j + depth) % depth, "up")
 
         @pl.loop(0, 8)
         def _(i):
@@ -189,22 +211,11 @@
             def _():
                 at = (zz + depth) % depth
 
-                @pl.when(d > 0)
-                def _():
-                    @pl.loop(0, ROWS_Y)
-                    def _(j):
-                        b = blk(at, (y + j) % ROWS_Y, c)
-                        landed(b, 0, ey.at[b])
-
-                        @pl.when(jnp.logical_and(sign == 1, z > 0))
-                        def _():
-                            copy("dn", b, 0, ey.at[b]).start()
-
-                        @pl.when(jnp.logical_and(sign == 0, z < depth - 1))
-                        def _():
-                            copy("up", b, 0, ey.at[b]).start()
-
-                        copy("d2d", b, 0, ey.at[b]).start()
+                end = jnp.logical_or(jnp.logical_and(sign == 1, z == 0), jnp.logical_and(sign == 0, z == depth - 1))
+
+                @pl.when(jnp.logical_and(d > 0, end))
+                def _():
+                    pass_first(at, None)
 
                 @pl.loop(0, ROWS_Y)
                 def _(yy):
@@ -281,9 +292,13 @@
             sent("up", 0, ey.at[b])
 
 
+def head_rows(rows):
+    return rows * 3 // 16
+
+
 def fused(n, elements, w_screened, coulomb):
     rows, cols = elements.shape
-    head = rows // CHUNKS
+    head = head_rows(rows)
     depth = n // (ROWS_Y * CORES)
     f32 = jnp.float32
     half = n // CORES
@@ -339,7 +354,7 @@
         rows, cols = pair_elements.shape
         elements = jnp.take(pair_elements, gmap % rows, axis=0, mode="clip")
         held = 4 * n * rows * (cols + rows) + 4 * 3 * rows * cols
-        fits = held < VMEM_ROOM and n % (ROWS_Y * CORES) == 0 and rows % (8 * CHUNKS) == 0
+        fits = held < VMEM_ROOM and n % (ROWS_Y * CORES) == 0 and rows % 128 == 0 and (rows - head_rows(rows)) % (8 * (CHUNKS - 1)) == 0
         if fits:
             return fused(n, elements, w_screened, coulomb)
         return plain(elements, w_screened, coulomb)

time: 178 us -> 155 us (0.87)
  Pallas kernels: 168 us -> 146 us
    pallas_call x1, Pallas kernels: 168 us -> 146 us  [fused(): pl.pallas_call(functools.partial(kernel, depth), out_shape=(jax.ShapeDtyp...]
where the time goes in v2:
time: 155 us
  Pallas kernels  146 us (94%)
  local copies, waits for them, and re-layouts  7.64 us (5%)
    pallas_call x1, Pallas kernels, fused(): pl.pallas_call(functools.partial(kernel, depth), out_shape=(jax.ShapeDtyp...  146 us
    unnamed x5, local copies, waits for them, and re-layouts  3.33 us

profile of v2, /device:TPU:0, one launch (start us, length us, event | category | flops | bytes accessed | tf_op | source)
XLA Modules:
  0.0 155.1 jit_solution(1065740992095454081)
XLA Ops:
  0.6 0.0 copy-start
  0.6 0.8 add_select_fusion
  1.5 0.6 copy-done
  2.1 0.0 copy-start.1
  2.1 2.5 %gather_fusion = f32[384,1024]{1,0:T(8,128)} fusion(f32[384,1024]{1,0:T(8,128)S(1)} %copy-done, s32[1024]{0:T(1024)S(1)} %pad_clamp_fusion), kind=kCustom, calls=%fused_computation | custom fusion | bytes 3147264 | tf_op jit(solution)/shard_map/jit(_take)/gather | solution.py:355
  4.5 0.0 copy-done.1
  4.5 0.6 reshape.13.c_ref
  5.1 146.0 %gather_matmul.1 = (f32[384,1024]{1,0:T(8,128)}, f32[1,1024]{1,0:T(1,128)}) custom-call(f32[384,1024]{1,0:T(8,128)} %gather_fusion, f32[16,384,384]{2,1,0:T(8,128)} %bitcast.3, f32[1,384]{1,0:T(1,128)} %reshape.13.c_ref), custom_call_target="tpu_custom_call" | custom-call | tf_op jit(solution)/shard_map/gather_matmul/pallas_call | solution.py:306
  151.1 1.3 dynamic-slice_bitcast_fusion
  152.4 2.7 %copy.7 = f32[384,1024]{1,0:T(8,128)} copy(f32[384,1024]{1,0:T(8,128)} %get-tuple-element.8) | data formatting | bytes 3145728
  (1 shorter events, 0.0 us)
Async XLA Ops:
  0.6 1.4 copy-start
  2.1 2.5 %copy-start.1 = (f32[384]{0:T(512)S(1)}, f32[384]{0:T(512)}, u32[]{:S(2)}) copy-start(f32[384]{0:T(512)} %param.7) | copy-start | bytes 4612
